TPU v7x, 32 devices: a whole 2x2x4 slice. The times are simulated.
32 devices in a mesh: groups: 2 (over y), expert: 8 (over z, core), dp: 2 (over x).
Axes of the slice: x: 2, y: 2, z: 4, core: 2. Of those that a mesh axis runs over, the one named last changes fastest.
Arguments:
- tokens: bfloat16 [1024, 2048], P(('groups', 'expert'), 'dp'), parts along dimension 0, may hold values from -6 to 6
- expert_ids: int32 [1024, 8], P(('groups', 'expert')), parts along dimension 0, may hold values from 0 to 15, all different within a row; in each aligned block of 64 rows (0 to 63, 64 to 127, ...) at most 64 rows name the same one
- gate_levels: int32 [1024, 8], P(('groups', 'expert')), parts along dimension 0, may hold values from 1 to 255
- gate_weight: bfloat16 [16, 2048, 1536], P('expert', None, 'dp'), may hold values from -0.125 to 0.125
- up_weight: bfloat16 [16, 2048, 1536], P('expert', None, 'dp'), may hold values from -0.125 to 0.125
- down_weight: bfloat16 [16, 1536, 2048], P('expert', None, 'dp'), may hold values from -0.15625 to 0.15625
Outputs:
- mixed: bfloat16 [1024, 2048], P(('groups', 'expert'), 'dp'), parts along dimension 0
There are 2 independent parts, one for each index of `groups`. A program takes and returns all parts, laid end to end along the dimension named above; an argument that names none is the same for every part. Nothing has to cross between parts.
Inputs may be any that keep to these rules, and one draw needn't show every extreme that they name: `expert_ids`: each row names 8 different experts. Among the rows of one index of the expert axis no expert is named more than 64 times, a bound that some block reaches.
All inputs are finite; a program needn't handle non-finite values.
Results may differ from a plain program's by a relative error of at most 0.0057.
Values may be sent and summed in bfloat16 or wider, within the bound.
A program may use at most 64 MiB of HBM per device.

v0:
```python
import jax
import jax.numpy as jnp
from jax import lax
from jax.sharding import PartitionSpec as P


def slot_numbers(chosen_ids, experts, capacity):
    flat_ids = chosen_ids.reshape(-1)
    labels = jnp.arange(experts, dtype=jnp.int32)
    onehot = (flat_ids[:, None] == labels[None, :]).astype(jnp.int32)
    before = jnp.cumsum(onehot, axis=0) - onehot
    position = jnp.sum(before * onehot, axis=1)
    return (flat_ids * capacity + position).reshape(chosen_ids.shape)


def route_matrix(slots, count):
    targets = jnp.arange(count, dtype=jnp.int32)
    return jnp.any(targets[:, None, None] == slots[None, :, :], axis=2).astype(jnp.bfloat16)


def on_device(tokens, expert_ids, gate_levels, gate_weight, up_weight, down_weight):
    tok_dev = tokens.shape[0]
    picks = expert_ids.shape[1]
    exp_dev = gate_weight.shape[0]
    n_expert = lax.axis_size("expert")
    experts = exp_dev * n_expert
    capacity = min(tok_dev, max(2, 2 * tok_dev * picks // experts))
    slot_count = experts * capacity
    own_slots = slot_numbers(expert_ids, experts, capacity)
    route = route_matrix(own_slots, slot_count)
    whole = lax.all_gather(tokens, "dp", axis=1, tiled=True)
    outgoing = jnp.dot(route, whole, preferred_element_type=jnp.float32).astype(jnp.bfloat16)
    outgoing = outgoing.reshape(n_expert, exp_dev, capacity, whole.shape[1])
    arrived = lax.all_to_all(outgoing, "expert", split_axis=0, concat_axis=0, tiled=True)
    gate_part = jnp.einsum(
        "sxcd,xdf->sxcf", arrived, gate_weight, preferred_element_type=jnp.float32
    )
    up_part = jnp.einsum("sxcd,xdf->sxcf", arrived, up_weight, preferred_element_type=jnp.float32)
    hidden = (jax.nn.silu(gate_part) * up_part).astype(jnp.bfloat16)
    out_features = down_weight.shape[2]
    outputs = jnp.einsum(
        "sxcf,xfk->sxck",
        lax.all_gather(hidden, "dp", axis=3, tiled=True),
        down_weight,
        preferred_element_type=jnp.float32,
    )
    result = outputs.astype(jnp.bfloat16)
    returned = lax.all_to_all(result, "expert", split_axis=0, concat_axis=0, tiled=True)
    returned = returned.reshape(slot_count, out_features)
    shares = gate_levels.astype(jnp.float32) / 256.0
    targets = jnp.arange(slot_count, dtype=jnp.int32)
    weighting = jnp.sum(
        jnp.where(
            targets[None, :, None] == own_slots[:, None, :], shares[:, None, :], jnp.float32(0.0)
        ),
        axis=2,
    )
    weighting = weighting.astype(jnp.bfloat16)
    combined = jnp.dot(weighting, returned, preferred_element_type=jnp.float32)
    return combined.astype(jnp.bfloat16)


def solution(mesh):
    in_specs = (
        P(("groups", "expert"), "dp"),
        P(("groups", "expert"), None),
        P(("groups", "expert"), None),
        P("expert", None, "dp"),
        P("expert", None, "dp"),
        P("expert", None, "dp"),
    )
    out_specs = P(("groups", "expert"), "dp")
    return jax.shard_map(
        on_device, mesh=mesh, in_specs=in_specs, out_specs=out_specs, check_vma=False
    )
```

profile of v0, /device:TPU:0, one launch (start us, length us, event | category | flops | bytes accessed | tf_op | source)
XLA Modules:
  0.0 241.4 jit_solution(17744205040662272902)
XLA Ops:
  6.5 0.8 copy.37
  7.3 0.1 eq.56
  7.4 0.1 eq.52
  7.5 1.2 reduce-window.6
  8.7 0.2 slice_reduce_fusion
  8.9 0.1 fusion.22
  9.0 0.1 reduce_sum.21
  9.1 0.1 copy.40
  9.2 0.7 multiply_add_fusion
  9.9 0.1 copy.41
  10.0 0.7 fusion.12
  10.7 7.4 %all_gather.6 = bf16[64,2048]{1,0:T(8,128)(2,1)S(1)} all-gather(bf16[64,1024]{1,0:T(8,128)(2,1)} %param.6), channel_id=1, replica_groups=mesh['groups'=2,'expert'=8,'dp'=2] {'dp'}, dimensions={1}, use_global_device_ids=true | all-gather | bytes 393216 | tf_op jit(solution)/shard_map/all_gather | solution.py:31
  18.1 1.3 convolution_convert_fusion
  19.4 99.1 %all_to_all.10 = bf16[8,2,64,2048]{3,2,1,0:T(8,128)(2,1)S(1)} all-to-all(bf16[8,2,64,2048]{3,2,1,0:T(8,128)(2,1)S(1)} %bitcast.64), channel_id=1, replica_groups=mesh['groups'=2,'expert'=8,'dp'=2] {'expert'}, dimensions={0} | all-to-all | bytes 8388608 | tf_op jit(solution)/shard_map/all_to_all | solution.py:34
  118.5 3.5 %fusion.2 = f32[2,8,64,768]{3,2,1,0:T(8,128)S(1)} fusion(bf16[2,2048,768]{2,1,0:T(8,128)(2,1)S(1)} %bitcast.67, bf16[8,2,64,2048]{3,2,1,0:T(8,128)(2,1)S(1)} %all_to_all.10), kind=kOutput, calls=%fused_computation.2 | convolution fusion | flops 3221225472 | bytes 13631488 | tf_op jit(solution)/shard_map/sxcd,xdf->sxcf/dot_general | solution.py:38
  122.0 4.9 %fusion.8 = bf16[8,2,64,768]{3,2,0,1:T(8,128)(2,1)} fusion(f32[2,8,64,768]{3,2,1,0:T(8,128)S(1)} %fusion.2, bf16[2,2048,768]{2,1,0:T(8,128)(2,1)S(1)} %bitcast.69, bf16[8,2,64,2048]{3,2,1,0:T(8,128)(2,1)S(1)} %all_to_all.10), kind=kOutput, calls=%fused_computation.10 | convolution fusion | flops 3225944064 | bytes 15204352 | tf_op jit(solution)/shard_map/sxcd,xdf->sxcf/dot_general | solution.py:35
  126.9 44.0 %all-gather.2.cloned.1.call-done = bf16[8,2,64,1536]{3,2,0,1:T(8,128)(2,1)} async-done(((bf16[8,2,64,768]{3,2,0,1:T(8,128)(2,1)}), bf16[8,2,64,1536]{3,2,0,1:T(8,128)(2,1)}) %all-gather.2.cloned.1.call-update) | async-done | bytes 3145744 | tf_op jit(solution)/shard_map/all_gather | solution.py:43
  170.9 7.2 %convert_bitcast_fusion = bf16[8,2,64,1024]{3,2,0,1:T(8,128)(2,1)S(1)} fusion(bf16[8,2,64,1536]{3,2,0,1:T(8,128)(2,1)} %all-gather.2.cloned.1.call-done, bf16[2,1536,1024]{2,1,0:T(8,128)(2,1)} %param.11), kind=kOutput, calls=%fused_computation.16 | convolution fusion | flops 3222274048 | bytes 11534336 | tf_op jit(solution)/shard_map/sxcf,xfk->sxck/dot_general | solution.py:41
  178.1 1.6 copy.46
  179.6 4.7 %all-to-all-start.1 = ((bf16[8,2,64,1024]{3,2,1,0:T(8,128)(2,1)}), bf16[8,2,64,1024]{3,2,1,0:T(8,128)(2,1)S(1)}, u32[]{:S(2)}, u32[]{:S(2)}) async-start(bf16[8,2,64,1024]{3,2,1,0:T(8,128)(2,1)} %copy.46), calls=%async_computation.1 | async-start | bytes 4194304 | tf_op jit(solution)/shard_map/all_to_all | solution.py:48
  184.4 0.1 copy.42
  184.5 0.7 select_reduce_fusion
  185.2 48.2 %all-to-all-done.1 = bf16[8,2,64,1024]{3,2,1,0:T(8,128)(2,1)S(1)} async-done(((bf16[8,2,64,1024]{3,2,1,0:T(8,128)(2,1)}), bf16[8,2,64,1024]{3,2,1,0:T(8,128)(2,1)S(1)}, u32[]{:S(2)}, u32[]{:S(2)}) %all-to-all-start.1) | async-done | bytes 2097184 | tf_op jit(solution)/shard_map/all_to_all | solution.py:48
  233.4 1.1 convolution_convert_fusion.1
  (18 shorter events, 0.1 us)
Async XLA Ops:
  6.5 164.4 %all-gather.2.cloned.1.call-start = ((), (), s32[]{:S(2)}) async-start(), calls=%async_computation.2 | async-start | bytes 4718592 | tf_op jit(solution)/shard_map/all_gather | solution.py:43
  18.1 100.4 %slice-start = ((s8[6291456]{0:T(1024)(128)(4,1)}), s8[4194304]{0:T(1024)(128)(4,1)S(1)}, s32[]{:S(2)}) async-start(s8[6291456]{0:T(1024)(128)(4,1)} %bitcast.66), calls=%async_computation.3 | async-start | bytes 8388608
  19.4 99.1 %slice-start.1 = ((s8[6291456]{0:T(1024)(128)(4,1)}), s8[2097152]{0:T(1024)(128)(4,1)S(1)}, s32[]{:S(2)}) async-start(s8[6291456]{0:T(1024)(128)(4,1)} %bitcast.66), calls=%async_computation.4 | async-start | bytes 4194304
  19.4 102.6 %slice-start.2 = ((s8[6291456]{0:T(1024)(128)(4,1)}), s8[4194304]{0:T(1024)(128)(4,1)S(1)}, s32[]{:S(2)}) async-start(s8[6291456]{0:T(1024)(128)(4,1)} %bitcast.68), calls=%async_computation.5 | async-start | bytes 8388608
  118.5 3.5 %slice-start.3 = ((s8[6291456]{0:T(1024)(128)(4,1)}), s8[2097152]{0:T(1024)(128)(4,1)S(1)}, s32[]{:S(2)}) async-start(s8[6291456]{0:T(1024)(128)(4,1)} %bitcast.68), calls=%async_computation.6 | async-start | bytes 4194304
  179.6 4.7 %copy-start = (s32[64,8]{0,1:T(8,128)S(1)}, s32[64,8]{0,1:T(8,128)}, u32[]{:S(2)}) copy-start(s32[64,8]{0,1:T(8,128)} %param.8) | copy-start | bytes 6148
  179.6 53.8 %all-to-all-start.1 = ((bf16[8,2,64,1024]{3,2,1,0:T(8,128)(2,1)}), bf16[8,2,64,1024]{3,2,1,0:T(8,128)(2,1)S(1)}, u32[]{:S(2)}, u32[]{:S(2)}) async-start(bf16[8,2,64,1024]{3,2,1,0:T(8,128)(2,1)} %copy.46), calls=%async_computation.1 | async-start | bytes 4194304 | tf_op jit(solution)/shard_map/all_to_all | solution.py:48
Sparse Core Ops, SparseCore 0:
  127.0 43.8 all-gather.1
where the time goes:
time: 242 us; the launch traced here: 241 us
  blocking collectives  107 us (44%)
  waiting for transfers between devices  92.2 us (38%)
  matrix products  17.9 us (7%)
  between operations  13.5 us (6%)
  starting transfers between devices  4.74 us (2%)
  other arithmetic  3.42 us (1%)
  local copies, waits for them, and re-layouts  3.08 us (1%)
    all_to_all x1, blocking collectives, on_device(): lax.all_to_all(outgoing, 'expert', split_axis=0, concat_axis=0, tiled=True)  99.1 us
    all_to_all x1, waiting for transfers between devices, on_device(): lax.all_to_all(result, 'expert', split_axis=0, concat_axis=0, tiled=True)  48.2 us
    all_gather x1, waiting for transfers between devices, on_device(): lax.all_gather(hidden, 'dp', axis=3, tiled=True)  44 us
    all_gather x1, blocking collectives, on_device(): whole = lax.all_gather(tokens, 'dp', axis=1, tiled=True)  7.39 us
    dot_general x1, matrix products, on_device(): jnp.einsum('sxcf,xfk->sxck', lax.all_gather(hidden, 'dp', axis=3, tiled=T...  7.15 us
    dot_general x1, matrix products, on_device(): jnp.einsum('sxcd,xdf->sxcf', arrived, gate_weight, preferred_element_type...  4.87 us
  transfers between devices with their start and end apart: 2, of which 2 were waited for; matrix products, arithmetic and copies ran while one was open for 0% of the time, Pallas kernels for 0%

commit v1 on v0

--- a/solution.py
+++ b/solution.py
@@ -38,12 +38,26 @@
     up_part = jnp.einsum("sxcd,xdf->sxcf", arrived, up_weight, preferred_element_type=jnp.float32)
     hidden = (jax.nn.silu(gate_part) * up_part).astype(jnp.bfloat16)
     out_features = down_weight.shape[2]
+    size, index = (lax.axis_size("dp"), lax.axis_index("dp"))
+    left = [(i, (i - 1) % size) for i in range(size)]
+    extent = hidden.shape[3]
+    held = hidden
     outputs = jnp.einsum(
         "sxcf,xfk->sxck",
-        lax.all_gather(hidden, "dp", axis=3, tiled=True),
-        down_weight,
+        held,
+        lax.dynamic_slice_in_dim(down_weight, index * extent, held.shape[3], axis=1),
         preferred_element_type=jnp.float32,
     )
+    for step in range(1, size):
+        held = lax.ppermute(held, "dp", left)
+        outputs = outputs + jnp.einsum(
+            "sxcf,xfk->sxck",
+            held,
+            lax.dynamic_slice_in_dim(
+                down_weight, (index + step) % size * extent, held.shape[3], axis=1
+            ),
+            preferred_element_type=jnp.float32,
+        )
     result = outputs.astype(jnp.bfloat16)
     returned = lax.all_to_all(result, "expert", split_axis=0, concat_axis=0, tiled=True)
     returned = returned.reshape(slot_count, out_features)

time: 242 us -> 215 us (0.89)
  waiting for transfers between devices: 92.2 us -> 78.7 us
  between operations: 13.5 us -> 0.14 us
    all_gather x1 -> x0, waiting for transfers between devices: 44 us -> none  [on_device(): lax.all_gather(hidden, 'dp', axis=3, tiled=True)]
    ppermute x0 -> x1, waiting for transfers between devices: none -> 30.6 us  [on_device(): held = lax.ppermute(held, 'dp', left)]
    dot_general x1 -> x2, matrix products: 7.15 us -> 7.41 us  [on_device(): jnp.einsum('sxcf,xfk->sxck', held, lax.dynamic_slice_in_dim(down_weight,...]
  transfers between devices with their start and end apart: 2 -> 2, of which waited for: 2 -> 2; matrix products, arithmetic and copies ran while one was open for 0% -> 2% of each run, Pallas kernels for 0% -> 0%
where the time goes in v1:
time: 215 us; the launch traced here: 214 us
  blocking collectives  107 us (50%)
  waiting for transfers between devices  78.7 us (37%)
  matrix products  17.2 us (8%)
  starting transfers between devices  5.29 us (2%)
  other arithmetic  3.42 us (2%)
  local copies, waits for them, and re-layouts  3.09 us (1%)
    all_to_all x1, blocking collectives, on_device(): lax.all_to_all(outgoing, 'expert', split_axis=0, concat_axis=0, tiled=True)  99.1 us
    all_to_all x1, waiting for transfers between devices, on_device(): lax.all_to_all(result, 'expert', split_axis=0, concat_axis=0, tiled=True)  48.1 us
    ppermute x1, waiting for transfers between devices, on_device(): held = lax.ppermute(held, 'dp', left)  30.6 us
    dot_general x2, matrix products, on_device(): jnp.einsum('sxcf,xfk->sxck', held, lax.dynamic_slice_in_dim(down_weight,...  7.41 us
    all_gather x1, blocking collectives, on_device(): whole = lax.all_gather(tokens, 'dp', axis=1, tiled=True)  7.39 us
  transfers between devices with their start and end apart: 2, of which 2 were waited for; matrix products, arithmetic and copies ran while one was open for 2% of the time, Pallas kernels for 0%

profile of v1, /device:TPU:0, one launch (start us, length us, event | category | flops | bytes accessed | tf_op | source)
XLA Modules:
  0.0 214.3 jit_solution(309224287259834791)
XLA Ops:
  0.0 0.8 copy.37
  0.8 0.1 eq.54
  0.9 0.1 eq.58
  1.0 1.2 reduce-window.6
  2.1 0.2 slice_reduce_fusion
  2.4 0.1 fusion.27
  2.5 0.1 reduce_sum.21
  2.6 0.7 multiply_add_fusion
  3.3 0.1 copy.41
  3.4 0.7 fusion.17
  4.1 7.4 %all_gather.3 = bf16[64,2048]{1,0:T(8,128)(2,1)S(1)} all-gather(bf16[64,1024]{1,0:T(8,128)(2,1)} %param.6), channel_id=1, replica_groups=mesh['groups'=2,'expert'=8,'dp'=2] {'dp'}, dimensions={1}, use_global_device_ids=true | all-gather | bytes 393216 | tf_op jit(solution)/shard_map/all_gather | solution.py:31
  11.5 1.3 convolution_convert_fusion
  12.9 99.1 %all_to_all.10 = bf16[8,2,64,2048]{3,2,1,0:T(8,128)(2,1)S(1)} all-to-all(bf16[8,2,64,2048]{3,2,1,0:T(8,128)(2,1)S(1)} %bitcast.70), channel_id=1, replica_groups=mesh['groups'=2,'expert'=8,'dp'=2] {'expert'}, dimensions={0} | all-to-all | bytes 8388608 | tf_op jit(solution)/shard_map/all_to_all | solution.py:34
  112.0 3.5 %fusion = f32[2,8,64,768]{3,2,1,0:T(8,128)S(1)} fusion(bf16[2,2048,768]{2,1,0:T(8,128)(2,1)S(1)} %bitcast.73, bf16[8,2,64,2048]{3,2,1,0:T(8,128)(2,1)S(1)} %all_to_all.10), kind=kOutput, calls=%fused_computation | convolution fusion | flops 3221225472 | bytes 13631488 | tf_op jit(solution)/shard_map/sxcd,xdf->sxcf/dot_general | solution.py:38
  115.5 3.9 %fusion.10 = bf16[8,2,64,768]{3,2,0,1:T(8,128)(2,1)S(1)} fusion(f32[2,8,64,768]{3,2,1,0:T(8,128)S(1)} %fusion, bf16[2,2048,768]{2,1,0:T(8,128)(2,1)S(1)} %bitcast.75, bf16[8,2,64,2048]{3,2,1,0:T(8,128)(2,1)S(1)} %all_to_all.10), kind=kOutput, calls=%fused_computation.13 | convolution fusion | flops 3225944064 | bytes 15204352 | tf_op jit(solution)/shard_map/sxcd,xdf->sxcf/dot_general | solution.py:35
  119.3 1.6 collective-permute-start
  120.9 3.7 %fusion.8 = f32[2,1024,8,64]{1,3,2,0:T(8,128)S(1)} fusion(bf16[8,2,64,768]{3,2,0,1:T(8,128)(2,1)S(1)} %fusion.10, bf16[2,1536,1024]{2,1,0:T(8,128)(2,1)} %param.11, s32[]{:T(128)S(6)} %select_n.18), kind=kOutput, calls=%fused_computation.10 | convolution fusion | flops 1610612736 | bytes 8912900 | tf_op jit(solution)/shard_map/sxcf,xfk->sxck/dot_general | solution.py:45
  124.6 30.6 %collective-permute-done = bf16[8,2,64,768]{3,2,0,1:T(8,128)(2,1)S(1)} collective-permute-done((bf16[8,2,64,768]{3,2,0,1:T(8,128)(2,1)S(1)}, bf16[8,2,64,768]{3,2,0,1:T(8,128)(2,1)S(1)}, u32[]{:S(2)}, u32[]{:S(2)}) %collective-permute-start) | collective-permute-done | bytes 1572896 | tf_op jit(solution)/shard_map/ppermute | solution.py:52
  155.2 3.7 %fusion.16 = bf16[8,2,64,1024]{3,2,0,1:T(8,128)(2,1)S(1)} fusion(f32[2,1024,8,64]{1,3,2,0:T(8,128)S(1)} %fusion.8, bf16[8,2,64,768]{3,2,0,1:T(8,128)(2,1)S(1)} %collective-permute-done, bf16[2,1536,1024]{2,1,0:T(8,128)(2,1)} %param.11, s32[]{:T(128)S(6)} %select_n.20), kind=kOutput, calls=%fused_computation.21 | convolution fusion | flops 1612709888 | bytes 11010052 | tf_op jit(solution)/shard_map/sxcf,xfk->sxck/dot_general | solution.py:53
  158.9 1.6 copy.46
  160.5 3.7 %all-to-all-start.1 = ((bf16[8,2,64,1024]{3,2,1,0:T(8,128)(2,1)}), bf16[8,2,64,1024]{3,2,1,0:T(8,128)(2,1)S(1)}, u32[]{:S(2)}, u32[]{:S(2)}) async-start(bf16[8,2,64,1024]{3,2,1,0:T(8,128)(2,1)} %copy.46), calls=%async_computation.1 | async-start | bytes 4194304 | tf_op jit(solution)/shard_map/all_to_all | solution.py:62
  164.3 0.7 select_reduce_fusion
  165.1 48.1 %all-to-all-done.1 = bf16[8,2,64,1024]{3,2,1,0:T(8,128)(2,1)S(1)} async-done(((bf16[8,2,64,1024]{3,2,1,0:T(8,128)(2,1)}), bf16[8,2,64,1024]{3,2,1,0:T(8,128)(2,1)S(1)}, u32[]{:S(2)}, u32[]{:S(2)}) %all-to-all-start.1) | async-done | bytes 2097184 | tf_op jit(solution)/shard_map/all_to_all | solution.py:62
  213.2 1.1 convolution_convert_fusion.1
  (18 shorter events, 0.2 us)
Async XLA Ops:
  11.5 100.4 %slice-start = ((s8[6291456]{0:T(1024)(128)(4,1)}), s8[4194304]{0:T(1024)(128)(4,1)S(1)}, s32[]{:S(2)}) async-start(s8[6291456]{0:T(1024)(128)(4,1)} %bitcast.72), calls=%async_computation.2 | async-start | bytes 8388608
  12.8 99.1 %slice-start.1 = ((s8[6291456]{0:T(1024)(128)(4,1)}), s8[2097152]{0:T(1024)(128)(4,1)S(1)}, s32[]{:S(2)}) async-start(s8[6291456]{0:T(1024)(128)(4,1)} %bitcast.72), calls=%async_computation.3 | async-start | bytes 4194304
  12.8 102.6 %slice-start.2 = ((s8[6291456]{0:T(1024)(128)(4,1)}), s8[4194304]{0:T(1024)(128)(4,1)S(1)}, s32[]{:S(2)}) async-start(s8[6291456]{0:T(1024)(128)(4,1)} %bitcast.74), calls=%async_computation.4 | async-start | bytes 8388608
  112.0 3.5 %slice-start.3 = ((s8[6291456]{0:T(1024)(128)(4,1)}), s8[2097152]{0:T(1024)(128)(4,1)S(1)}, s32[]{:S(2)}) async-start(s8[6291456]{0:T(1024)(128)(4,1)} %bitcast.74), calls=%async_computation.5 | async-start | bytes 4194304
  119.3 35.8 %collective-permute-start = (bf16[8,2,64,768]{3,2,0,1:T(8,128)(2,1)S(1)}, bf16[8,2,64,768]{3,2,0,1:T(8,128)(2,1)S(1)}, u32[]{:S(2)}, u32[]{:S(2)}) collective-permute-start(bf16[8,2,64,768]{3,2,0,1:T(8,128)(2,1)S(1)} %fusion.10), channel_id=1, source_target_pairs={{0,1},{1,0},{2,3},{3,2},{4,5},{5,4},{6,7},{7,6},{8,9},{9,8},{10,11... | collective-permute-start | bytes 4718600 | tf_op jit(solution)/shard_map/ppermute | solution.py:52
  160.5 3.7 %copy-start = (s32[64,8]{0,1:T(8,128)S(1)}, s32[64,8]{0,1:T(8,128)}, u32[]{:S(2)}) copy-start(s32[64,8]{0,1:T(8,128)} %param.8) | copy-start | bytes 6148
  160.5 52.7 %all-to-all-start.1 = ((bf16[8,2,64,1024]{3,2,1,0:T(8,128)(2,1)}), bf16[8,2,64,1024]{3,2,1,0:T(8,128)(2,1)S(1)}, u32[]{:S(2)}, u32[]{:S(2)}) async-start(bf16[8,2,64,1024]{3,2,1,0:T(8,128)(2,1)} %copy.46), calls=%async_computation.1 | async-start | bytes 4194304 | tf_op jit(solution)/shard_map/all_to_all | solution.py:62
